TPU v7x, 32 devices: a whole 2x2x4 slice. The times are simulated.
32 devices in a mesh: members: 2 (over y), band: 4 (over z), head: 4 (over x, core).
Axes of the slice: x: 2, y: 2, z: 4, core: 2. Of those that a mesh axis runs over, the one named last changes fastest.
Arguments:
- grid_feats: bfloat16 [4096, 1024], P(('members', 'band')), parts along dimension 0, may hold values from -6 to 6
- mesh_feats: bfloat16 [4096, 1024], P(('members', 'band')), parts along dimension 0, may hold values from -6 to 6
- enc_in: bfloat16 [3, 1024, 1024], P(None, 'band', 'head'), may hold values from -0.19921875 to 0.19921875
- enc_out: bfloat16 [1024, 1024], P('head', 'band'), may hold values from -0.1875 to 0.1875
- proc_in: bfloat16 [3, 1024, 1024], P(None, 'band', 'head'), may hold values from -0.19921875 to 0.19921875
- proc_out: bfloat16 [1024, 1024], P('head', 'band'), may hold values from -0.1875 to 0.1875
- ff_up: bfloat16 [1024, 4096], P('band', 'head'), may hold values from -0.1875 to 0.1875
- ff_down: bfloat16 [4096, 1024], P('head', 'band'), may hold values from -0.09375 to 0.09375
- dec_in: bfloat16 [3, 1024, 1024], P(None, 'band', 'head'), may hold values from -0.19921875 to 0.19921875
- dec_out: bfloat16 [1024, 1024], P('head', 'band'), may hold values from -0.1875 to 0.1875
- enc_list: int32 [16, 8], replicated, may hold values from 0 to 15, as said below
- enc_count: int32 [16], replicated, may hold values from 1 to 8
- dec_list: int32 [16, 8], replicated, may hold values from 0 to 15, as said below
- dec_count: int32 [16], replicated, may hold values from 1 to 8
- window_ids: int32 [2048], replicated, may hold values from 0 to 1, never falling along the last dimension, each value on 1 to 1536 neighbouring positions
Outputs:
- grid_out: bfloat16 [4096, 1024], P(('members', 'band', 'head')), parts along dimension 0
There are 2 independent parts, one for each index of `members`. A program takes and returns all parts, laid end to end along the dimension named above; an argument that names none is the same for every part. Nothing has to cross between parts.
Inputs may be any that keep to these rules, and one draw needn't show every extreme that they name: `enc_list`: each row holds distinct block numbers. Every block listed for mesh block m lies in the band of 512 grid points with the same band number as m's band of 512 nodes, or in the band just before or just after it. Only the first enc_count[m] slots of row m of enc_list are used. `dec_list`: each row holds distinct block numbers. Every block listed for grid block g lies in the band of 512 mesh nodes with the same band number as g's band of 512 grid points, or in the band just before or just after it. Only the first dec_count[g] slots of row g of dec_list are used. `window_ids`: never falls along the nodes; each window holds at most 1536 consecutive nodes.
All inputs are finite; a program needn't handle non-finite values.
Results may differ from a plain program's by a relative error of at most 0.02.
Values may be sent and summed in bfloat16 or wider, within the bound.
No kernel may reach another device: no remote copies, remote signals or barrier semaphores. Data moves between devices by JAX's collectives and lax.ppermute only.
A program may use at most 64 MiB of HBM per device.

v0:
```python
import jax
import jax.numpy as jnp
from jax import lax
from jax.sharding import PartitionSpec as P

HD = 64
BLOCK = 128
WINDOW = 1536
EPSILON = 1e-05
NEGATIVE = -1e30


def padded(block, sides, width):
    for axis, dim in sides:
        count = lax.axis_size(axis)
        forward = [(i, i + 1) for i in range(count - 1)]
        backward = [(target, source) for source, target in forward]
        low = lax.ppermute(
            lax.slice_in_dim(block, block.shape[dim] - width, None, axis=dim), axis, forward
        )
        high = lax.ppermute(lax.slice_in_dim(block, 0, width, axis=dim), axis, backward)
        block = jnp.concatenate([low, block, high], axis=dim)
    return block


def shifted(block, axis, distance):
    devices = range(lax.axis_size(axis))
    route = [(i - distance, i) for i in devices if i - distance in devices]
    return lax.ppermute(block, axis, route)


def normed(source):
    values_f = source.astype(jnp.float32)
    centred = values_f - jnp.mean(values_f, axis=-1, keepdims=True)
    variance = jnp.mean(centred * centred, axis=-1, keepdims=True)
    return (centred * lax.rsqrt(variance + EPSILON)).astype(jnp.bfloat16)


def fold_three(sources, carry, piece):
    width = piece.shape[1]
    return tuple(
        (
            total
            + jnp.dot(
                lax.slice_in_dim(source, 0, width, axis=1),
                piece[which],
                preferred_element_type=jnp.float32,
            )
            for which, (total, source) in enumerate(zip(carry, sources))
        )
    )


def fold_rows(source, total, piece):
    return total + jnp.dot(
        lax.slice_in_dim(source, 0, piece.shape[0], axis=1),
        piece,
        preferred_element_type=jnp.float32,
    )


def columns_of(source, piece):
    return jnp.dot(source, piece, preferred_element_type=jnp.float32)


def head_scores(queries, key_rows, head_index, allowed):
    lower = head_index * HD
    scores = jnp.einsum(
        "qd,kd->qk",
        queries[:, lower : lower + HD],
        key_rows[:, lower : lower + HD],
        preferred_element_type=jnp.float32,
    ) * HD ** (-0.5)
    scores = jnp.where(allowed, scores, NEGATIVE)
    maxima = jnp.max(scores, axis=1, keepdims=True)
    expo = jnp.where(allowed, jnp.exp(scores - maxima), 0.0)
    return (expo, maxima, jnp.sum(expo, axis=1, keepdims=True))


def attend_rounded(queries, key_rows, value_rows, allowed):
    outputs = []
    for head_index in range(queries.shape[1] // HD):
        expo, maxima, totals = head_scores(queries, key_rows, head_index, allowed)
        weights = (expo / totals).astype(jnp.bfloat16)
        lower = head_index * HD
        outputs.append(
            jnp.dot(weights, value_rows[:, lower : lower + HD], preferred_element_type=jnp.float32)
        )
    return jnp.concatenate(outputs, axis=1).astype(jnp.bfloat16)


def partial_attend(queries, key_rows, value_rows, allowed):
    outputs, maxima_all, totals_all = ([], [], [])
    for head_index in range(queries.shape[1] // HD):
        expo, maxima, totals = head_scores(queries, key_rows, head_index, allowed)
        lower = head_index * HD
        outputs.append(
            jnp.dot(
                expo,
                value_rows[:, lower : lower + HD].astype(jnp.float32),
                precision=lax.Precision.HIGHEST,
            )
        )
        maxima_all.append(maxima)
        totals_all.append(totals)
    return (
        jnp.concatenate(outputs, axis=1),
        jnp.concatenate(maxima_all, axis=1),
        jnp.concatenate(totals_all, axis=1),
    )


def listed_attend(queries, key_pool, value_pool, lists, counts, base_block, rounded):
    width = queries.shape[1]
    rows = queries.shape[0]
    pool_blocks = key_pool.shape[0] // BLOCK
    key_blocks = key_pool.reshape(pool_blocks, BLOCK, width)
    value_blocks = value_pool.reshape(pool_blocks, BLOCK, width)
    slots = lists.shape[1]

    def one_block(index):
        listed = lists[index] - base_block
        inside = (
            (listed >= 0)
            & (listed < pool_blocks)
            & (jnp.arange(slots, dtype=jnp.int32) < counts[index])
        )
        safe = jnp.clip(listed, 0, pool_blocks - 1)
        block_keys = key_blocks[safe].reshape(slots * BLOCK, width)
        block_values = value_blocks[safe].reshape(slots * BLOCK, width)
        allowed = jnp.repeat(inside, BLOCK)[None, :]
        block_queries = lax.dynamic_slice_in_dim(queries, index * BLOCK, BLOCK, 0)
        if rounded:
            return attend_rounded(block_queries, block_keys, block_values, allowed)
        return partial_attend(block_queries, block_keys, block_values, allowed)

    result = lax.map(one_block, jnp.arange(rows // BLOCK, dtype=jnp.int32))
    return jax.tree.map(lambda stacked: stacked.reshape(rows, stacked.shape[-1]), result)


def normalize(outputs, totals):
    rows = outputs.shape[0]
    heads_here = totals.shape[1]
    shaped = outputs.reshape(rows, heads_here, HD) / totals[:, :, None]
    return shaped.reshape(rows, heads_here * HD).astype(jnp.bfloat16)


def per_device(
    grid_feats,
    mesh_feats,
    enc_in,
    enc_out,
    proc_in,
    proc_out,
    ff_up,
    ff_down,
    dec_in,
    dec_out,
    enc_list,
    enc_count,
    dec_list,
    dec_count,
    window_ids,
):
    band_index = lax.axis_index("band")
    grid_rows = grid_feats.shape[0]
    mesh_rows = mesh_feats.shape[0]
    width = enc_in.shape[2]
    grid_blocks = grid_rows // BLOCK
    mesh_blocks = mesh_rows // BLOCK
    grid_norm = normed(grid_feats)
    mesh_norm = normed(mesh_feats)
    grid_zeros = jnp.zeros((grid_rows, width), jnp.float32)
    mesh_zeros = jnp.zeros((mesh_rows, width), jnp.float32)
    enc_q, enc_k, enc_v = fold_three(
        (mesh_norm, grid_norm, grid_norm),
        (mesh_zeros, grid_zeros, grid_zeros),
        lax.all_gather(enc_in, "band", axis=1, tiled=True),
    )
    enc_q = enc_q.astype(jnp.bfloat16)
    enc_k = enc_k.astype(jnp.bfloat16)
    enc_v = enc_v.astype(jnp.bfloat16)
    my_lists = lax.dynamic_slice_in_dim(enc_list, band_index * mesh_blocks, mesh_blocks, 0)
    my_counts = lax.dynamic_slice_in_dim(enc_count, band_index * mesh_blocks, mesh_blocks, 0)
    pool = padded(jnp.stack([enc_k, enc_v]), (("band", 1),), grid_rows)
    outputs, maxima, totals = listed_attend(
        enc_q, pool[0], pool[1], my_lists, my_counts, (band_index - 1) * grid_blocks, False
    )
    enc_attn = normalize(outputs, totals)
    enc_terms = columns_of(enc_attn, lax.all_gather(enc_out, "band", axis=1, tiled=True))
    mesh_state = mesh_feats.astype(jnp.float32) + lax.psum(
        enc_terms.astype(jnp.bfloat16), "head"
    ).astype(jnp.float32)
    proc_norm = normed(mesh_state)
    proc_q, proc_k, proc_v = fold_three(
        (proc_norm, proc_norm, proc_norm),
        (mesh_zeros, mesh_zeros, mesh_zeros),
        lax.all_gather(proc_in, "band", axis=1, tiled=True),
    )
    proc_q = proc_q.astype(jnp.bfloat16)
    pairs = jnp.stack([proc_k.astype(jnp.bfloat16), proc_v.astype(jnp.bfloat16)])
    reach = (WINDOW + mesh_rows - 2) // mesh_rows
    slab_parts = {0: pairs}
    for distance in range(1, reach + 1):
        for direction in (1, -1):
            slab_parts[direction * distance] = shifted(pairs, "band", -direction * distance)
    slab = jnp.concatenate([slab_parts[offset] for offset in range(-reach, reach + 1)], axis=1)
    padded_ids = jnp.pad(window_ids, (reach * mesh_rows, reach * mesh_rows), constant_values=-1)
    slab_ids = lax.dynamic_slice_in_dim(
        padded_ids, band_index * mesh_rows, (2 * reach + 1) * mesh_rows, 0
    )
    slab_start = (band_index - reach) * mesh_rows
    span = 2 * WINDOW

    def window_block(index):
        first = band_index * mesh_rows + index * BLOCK
        first_id = window_ids[first]
        window_start = jnp.sum((window_ids < first_id).astype(jnp.int32))
        local = window_start - slab_start
        block_keys = lax.dynamic_slice_in_dim(slab[0], local, span, 0)
        block_values = lax.dynamic_slice_in_dim(slab[1], local, span, 0)
        key_ids = lax.dynamic_slice_in_dim(slab_ids, local, span, 0)
        query_ids = lax.dynamic_slice_in_dim(window_ids, first, BLOCK, 0)
        block_queries = lax.dynamic_slice_in_dim(proc_q, index * BLOCK, BLOCK, 0)
        return attend_rounded(
            block_queries, block_keys, block_values, query_ids[:, None] == key_ids[None, :]
        )

    proc_attn = lax.map(window_block, jnp.arange(mesh_blocks, dtype=jnp.int32)).reshape(
        mesh_rows, width
    )
    proc_terms = columns_of(proc_attn, lax.all_gather(proc_out, "band", axis=1, tiled=True))
    mesh_mid = mesh_state + lax.psum(proc_terms.astype(jnp.bfloat16), "head").astype(jnp.float32)
    ff_norm = normed(mesh_mid)
    hidden = fold_rows(
        ff_norm,
        jnp.zeros((mesh_rows, ff_up.shape[1]), jnp.float32),
        lax.all_gather(ff_up, "band", axis=0, tiled=True),
    )
    hidden = jax.nn.gelu(hidden, approximate=False).astype(jnp.bfloat16)
    ff_terms = columns_of(hidden, lax.all_gather(ff_down, "band", axis=1, tiled=True))
    mesh_final = mesh_mid + lax.psum(ff_terms.astype(jnp.bfloat16), "head").astype(jnp.float32)
    final_norm = normed(mesh_final)
    dec_q, dec_k, dec_v = fold_three(
        (grid_norm, final_norm, final_norm),
        (grid_zeros, mesh_zeros, mesh_zeros),
        lax.all_gather(dec_in, "band", axis=1, tiled=True),
    )
    dec_q = dec_q.astype(jnp.bfloat16)
    dec_pool = padded(
        jnp.stack([dec_k.astype(jnp.bfloat16), dec_v.astype(jnp.bfloat16)]),
        (("band", 1),),
        mesh_rows,
    )
    grid_lists = lax.dynamic_slice_in_dim(dec_list, band_index * grid_blocks, grid_blocks, 0)
    grid_counts = lax.dynamic_slice_in_dim(dec_count, band_index * grid_blocks, grid_blocks, 0)
    dec_attn = listed_attend(
        dec_q,
        dec_pool[0],
        dec_pool[1],
        grid_lists,
        grid_counts,
        (band_index - 1) * mesh_blocks,
        True,
    )
    full_out = lax.all_gather(dec_out, "band", axis=1, tiled=True)
    share = grid_rows // lax.axis_size("head")
    summed = lax.psum_scatter(
        jnp.dot(
            lax.slice_in_dim(dec_attn, 0, share * lax.axis_size("head"), axis=0),
            full_out,
            preferred_element_type=jnp.float32,
        ).astype(jnp.bfloat16),
        "head",
        scatter_dimension=0,
        tiled=True,
    ).astype(jnp.float32)
    residual = lax.dynamic_slice_in_dim(
        grid_feats, lax.axis_index("head") * share, share, 0
    ).astype(jnp.float32)
    return (residual + summed).astype(jnp.bfloat16)


def solution(mesh):
    return jax.shard_map(
        per_device,
        mesh=mesh,
        in_specs=(
            P(("members", "band"), None),
            P(("members", "band"), None),
            P(None, "band", "head"),
            P("head", "band"),
            P(None, "band", "head"),
            P("head", "band"),
            P("band", "head"),
            P("head", "band"),
            P(None, "band", "head"),
            P("head", "band"),
            P(),
            P(),
            P(),
            P(),
            P(),
        ),
        out_specs=P(("members", "band", "head"), None),
        check_vma=False,
    )
```

profile of v0, /device:TPU:0, one launch (start us, length us, event | category | flops | bytes accessed | tf_op | source)
XLA Modules:
  0.0 741.7 jit_solution(13681533981195559671)
XLA Ops:
  9.9 22.7 %all_gather.26 = bf16[256,1024]{1,0:T(8,128)(2,1)} all-gather(bf16[256,256]{1,0:T(8,128)(2,1)S(1)} %copy-done.19), channel_id=1, replica_groups=mesh['members'=2,'band'=4,'head'=4] {'band'}, dimensions={1}, use_global_device_ids=true | all-gather | bytes 655360 | tf_op jit(solution)/shard_map/all_gather | solution.py:190
  32.6 19.2 %all-gather.8.cloned.1.call-done = bf16[3,1024,256]{2,1,0:T(8,128)(2,1)} async-done(((bf16[3,256,256]{2,1,0:T(8,128)(2,1)}), bf16[3,1024,256]{2,1,0:T(8,128)(2,1)}) %all-gather.8.cloned.1.call-update) | async-done | bytes 1572880 | tf_op jit(solution)/shard_map/all_gather | solution.py:178
  54.9 3.3 collective-permute-start
  62.0 7.4 collective-permute-done
  69.4 4.1 collective-permute-done.1
  74.6 59.4 %while.34 = (s32[]{:T(128)}, f32[4,128,256]{2,1,0:T(8,128)}, f32[4,128,4]{1,2,0:T(4,128)S(1)}, s32[4]{0:T(128)S(1)}, s32[4,8]{1,0:T(4,128)S(1)}, /*index=5*/s32[...) while((s32[]{:T(128)}, f32[4,128,256]{2,1,0:T(8,128)}, ...), condition=%wide.region_13.14_spmd, body=%wide.region_4.13_spmd.sunk | while | flops 474056288 | bytes 11562037 | solution.py:137
  137.8 34.9 %all-reduce.5.cloned.1.call-done = bf16[512,1024]{1,0:T(8,128)(2,1)} async-done(((bf16[512,1024]{1,0:T(8,128)(2,1)}), bf16[512,1024]{1,0:T(8,128)(2,1)}) %all-reduce.5.cloned.1.call-update) | async-done | bytes 1048592 | tf_op jit(solution)/shard_map/psum | solution.py:191
  175.3 36.5 %all-gather.10.cloned.1.call-done = bf16[3,1024,256]{2,1,0:T(8,128)(2,1)} async-done(((bf16[3,256,256]{2,1,0:T(8,128)(2,1)}), bf16[3,1024,256]{2,1,0:T(8,128)(2,1)}) %all-gather.10.cloned.1.call-update) | async-done | bytes 1572880 | tf_op jit(solution)/shard_map/all_gather | solution.py:198
  214.9 3.2 collective-permute-start.2
  219.4 47.1 %all_gather.28 = bf16[256,1024]{1,0:T(8,128)(2,1)} all-gather(bf16[256,256]{1,0:T(8,128)(2,1)S(1)} %copy-done.20), channel_id=1, replica_groups=mesh['members'=2,'band'=4,'head'=4] {'band'}, dimensions={1}, use_global_device_ids=true | all-gather | bytes 655360 | tf_op jit(solution)/shard_map/all_gather | solution.py:232
  275.1 2.8 collective-permute-done.4
  279.0 4.5 collective-permute-done.5
  283.5 33.7 %collective-permute-done.6 = bf16[2,512,256]{2,1,0:T(8,128)(2,1)S(1)} collective-permute-done((bf16[2,512,256]{2,1,0:T(8,128)(2,1)S(1)}, bf16[2,512,256]{2,1,0:T(8,128)(2,1)S(1)}, u32[]{:S(2)}, u32[]{:S(2)}) %collective-permute-start.6) | collective-permute-done | bytes 524320 | tf_op jit(solution)/shard_map/ppermute | solution.py:29
  319.1 92.2 %while.35 = (s32[]{:T(128)}, bf16[4,128,256]{2,1,0:T(8,128)(2,1)S(1)}, s32[4]{0:T(128)S(1)}, s32[]{:T(128)}, s32[2048]{0:T(1024)S(1)}, /*index=5*/s32[]{:T(128)}...) while((s32[]{:T(128)}, ...), condition=%wide.region_27.28_spmd, body=%wide.region_17.27_spmd.sunk | while | flops 422220800 | bytes 58421236 | solution.py:229
  334.7 3.4 fusion.299
  351.5 2.5 fusion.298
  357.8 3.4 fusion.299
  374.6 2.5 fusion.298
  380.9 3.4 fusion.299
  403.9 3.4 fusion.299
  411.3 2.6 convolution_convert_fusion.10
  415.3 33.3 %all-reduce.7.cloned.1.call-done = bf16[512,1024]{1,0:T(8,128)(2,1)} async-done(((bf16[512,1024]{1,0:T(8,128)(2,1)}), bf16[512,1024]{1,0:T(8,128)(2,1)}) %all-reduce.7.cloned.1.call-update) | async-done | bytes 1048592 | tf_op jit(solution)/shard_map/psum | solution.py:233
  451.1 45.2 %all-gather.12.cloned.1.call-done = bf16[1024,1024]{1,0:T(8,128)(2,1)} async-done(((bf16[256,1024]{1,0:T(8,128)(2,1)}), bf16[1024,1024]{1,0:T(8,128)(2,1)}) %all-gather.12.cloned.1.call-update) | async-done | bytes 2097168 | tf_op jit(solution)/shard_map/all_gather | solution.py:238
  496.3 46.5 %all-gather.14.cloned.1.call-done = bf16[1024,1024]{1,0:T(8,128)(2,1)} async-done(((bf16[1024,256]{1,0:T(8,128)(2,1)}), bf16[1024,1024]{1,0:T(8,128)(2,1)}) %all-gather.14.cloned.1.call-update) | async-done | bytes 2097168 | tf_op jit(solution)/shard_map/all_gather | solution.py:241
  542.8 9.5 %convolution_convert_fusion.9 = bf16[512,1024]{1,0:T(8,128)(2,1)} fusion(bf16[1024,1024]{1,0:T(8,128)(2,1)} %all-gather.14.cloned.1.call-done, bf16[1024,1024]{1,0:T(8,128)(2,1)} %all-gather.12.cloned.1.call-done, f32[512,1024]{1,0:T(8,128)S(1)} %get-tuple-element.283, f32[512]{0:T(512)S(1)} %add_rsqrt_fusion.1, f32[512]{0:T(512)S(1)} %broadcast_multiply_fusion.1), kind=kOutput, calls=%fused_computation.216 | convolution fusion | flops 2183659520 | bytes 7344128 | tf_op jit(solution)/shard_map/dot_general | solution.py:63
  553.2 33.8 %all-reduce.9.cloned.1.call-done = bf16[512,1024]{1,0:T(8,128)(2,1)} async-done(((bf16[512,1024]{1,0:T(8,128)(2,1)}), bf16[512,1024]{1,0:T(8,128)(2,1)}) %all-reduce.9.cloned.1.call-update) | async-done | bytes 1048592 | tf_op jit(solution)/shard_map/psum | solution.py:242
  589.5 36.6 %all-gather.6.cloned.1.call-done = bf16[3,1024,256]{2,1,0:T(8,128)(2,1)} async-done(((bf16[3,256,256]{2,1,0:T(8,128)(2,1)}), bf16[3,1024,256]{2,1,0:T(8,128)(2,1)}) %all-gather.6.cloned.1.call-update) | async-done | bytes 1572880 | tf_op jit(solution)/shard_map/all_gather | solution.py:247
  629.3 2.5 collective-permute-start.8
  634.5 25.3 %all_gather.31 = bf16[256,1024]{1,0:T(8,128)(2,1)} all-gather(bf16[256,256]{1,0:T(8,128)(2,1)S(1)} %copy-done.21), channel_id=1, replica_groups=mesh['members'=2,'band'=4,'head'=4] {'band'}, dimensions={1}, use_global_device_ids=true | all-gather | bytes 655360 | tf_op jit(solution)/shard_map/all_gather | solution.py:266
  662.3 45.1 %while.36 = (s32[]{:T(128)}, bf16[4,128,256]{2,1,0:T(8,128)(2,1)}, s32[4]{0:T(128)S(1)}, s32[4,8]{1,0:T(4,128)S(1)}, s32[]{:T(128)}, /*index=5*/s32[4]{0:T(128)}...) while((s32[]{:T(128)}, bf16[4,128,256]{2,1,0:T(8,128)(2,1)}, ...), condition=%wide.region_43.44_spmd, body=%wide.region_34.43_spmd.sunk | while | flops 139755616 | bytes 19489944 | solution.py:137
  707.4 2.6 convolution_convert_fusion.8
  710.0 23.3 %reduce-scatter.2.cloned.1.call-done = bf16[128,1024]{1,0:T(8,128)(2,1)} async-done(((bf16[512,1024]{1,0:T(8,128)(2,1)}), bf16[128,1024]{1,0:T(8,128)(2,1)}) %reduce-scatter.2.cloned.1.call-update) | async-done | bytes 262160 | tf_op jit(solution)/shard_map/reduce_scatter | solution.py:268
  (418 shorter events, 202.7 us)
Async XLA Ops:
  6.5 53.0 %copy-start = (s32[16,8]{0,1:T(8,128)S(1)}, s32[16,8]{0,1:T(8,128)}, u32[]{:S(2)}) copy-start(s32[16,8]{0,1:T(8,128)} %param.31) | copy-start | bytes 1540
  6.5 45.2 %all-gather.8.cloned.1.call-start = ((), (), s32[]{:S(2)}) async-start(), calls=%async_computation.2 | async-start | bytes 1966080 | tf_op jit(solution)/shard_map/all_gather | solution.py:178
  7.3 165.4 %all-reduce.5.cloned.1.call-start = ((), (), s32[]{:S(2)}) async-start(), calls=%async_computation.3 | async-start | bytes 2097152 | tf_op jit(solution)/shard_map/psum | solution.py:191
  53.3 6.4 copy-start.23
  54.9 14.5 %collective-permute-start = (bf16[2,512,256]{2,1,0:T(8,128)(2,1)S(1)}, bf16[2,512,256]{2,1,0:T(8,128)(2,1)S(1)}, u32[]{:S(2)}, u32[]{:S(2)}) collective-permute-start(bf16[2,512,256]{2,1,0:T(8,128)(2,1)S(1)} %pad_maximum_fusion.4), channel_id=1, source_target_pairs={{0,4},{4,8},{8,12},{1,5},{5,9},{9,13},{2,6},{6,10},{10,14},{3,7},{... | collective-permute-start | bytes 1572872 | tf_op jit(solution)/shard_map/ppermute | solution.py:18
  58.2 15.3 %collective-permute-start.1 = (bf16[2,512,256]{2,1,0:T(8,128)(2,1)S(1)}, bf16[2,512,256]{2,1,0:T(8,128)(2,1)S(1)}, u32[]{:S(2)}, u32[]{:S(2)}) collective-permute-start(bf16[2,512,256]{2,1,0:T(8,128)(2,1)S(1)} %pad_maximum_fusion.4), channel_id=1, source_target_pairs={{4,0},{8,4},{12,8},{5,1},{9,5},{13,9},{6,2},{10,6},{14,10},{7,3},{... | collective-permute-start | bytes 1572872 | tf_op jit(solution)/shard_map/ppermute | solution.py:21
  134.3 38.4 %copy-start.7 = (bf16[512,1024]{1,0:T(8,128)(2,1)S(1)}, bf16[512,1024]{1,0:T(8,128)(2,1)}, u32[]{:S(2)}) copy-start(bf16[512,1024]{1,0:T(8,128)(2,1)} %param.22) | copy-start | bytes 3145732
  137.0 74.8 %all-gather.10.cloned.1.call-start = ((), (), s32[]{:S(2)}) async-start(), calls=%async_computation.4 | async-start | bytes 1966080 | tf_op jit(solution)/shard_map/all_gather | solution.py:198
  137.7 311.0 %all-reduce.7.cloned.1.call-start = ((), (), s32[]{:S(2)}) async-start(), calls=%async_computation.5 | async-start | bytes 2097152 | tf_op jit(solution)/shard_map/psum | solution.py:233
  213.3 6.2 copy-start.20
  213.3 55.4 %copy-start.18 = (s32[2048]{0:T(1024)S(1)}, s32[2048]{0:T(1024)}, u32[]{:S(2)}) copy-start(s32[2048]{0:T(1024)} %param.35) | copy-start | bytes 24580
  214.9 58.6 %collective-permute-start.2 = (bf16[2,512,256]{2,1,0:T(8,128)(2,1)S(1)}, bf16[2,512,256]{2,1,0:T(8,128)(2,1)S(1)}, u32[]{:S(2)}, u32[]{:S(2)}) collective-permute-start(bf16[2,512,256]{2,1,0:T(8,128)(2,1)S(1)} %pad_maximum_fusion.5), channel_id=1, source_target_pairs={{0,12},{1,13},{2,14},{3,15},{16,28},{17,29},{18,30},{19,31}} | collective-permute-start | bytes 1572872 | tf_op jit(solution)/shard_map/ppermute | solution.py:29
  218.1 56.9 %collective-permute-start.3 = (bf16[2,512,256]{2,1,0:T(8,128)(2,1)S(1)}, bf16[2,512,256]{2,1,0:T(8,128)(2,1)S(1)}, u32[]{:S(2)}, u32[]{:S(2)}) collective-permute-start(bf16[2,512,256]{2,1,0:T(8,128)(2,1)S(1)} %pad_maximum_fusion.5), channel_id=1, source_target_pairs={{0,8},{4,12},{1,9},{5,13},{2,10},{6,14},{3,11},{7,15},{16,24},{20,... | collective-permute-start | bytes 1572872 | tf_op jit(solution)/shard_map/ppermute | solution.py:29
  266.5 11.3 %collective-permute-start.4 = (bf16[2,512,256]{2,1,0:T(8,128)(2,1)S(1)}, bf16[2,512,256]{2,1,0:T(8,128)(2,1)}, u32[]{:S(2)}, u32[]{:S(2)}) collective-permute-start(bf16[2,512,256]{2,1,0:T(8,128)(2,1)S(1)} %pad_maximum_fusion.5), channel_id=1, source_target_pairs={{0,4},{4,8},{8,12},{1,5},{5,9},{9,13},{2,6},{6,10},{10,14},{3,7},{... | collective-permute-start | bytes 1572872 | tf_op jit(solution)/shard_map/ppermute | solution.py:29
  268.7 14.7 %collective-permute-start.5 = (bf16[2,512,256]{2,1,0:T(8,128)(2,1)S(1)}, bf16[2,512,256]{2,1,0:T(8,128)(2,1)S(1)}, u32[]{:S(2)}, u32[]{:S(2)}) collective-permute-start(bf16[2,512,256]{2,1,0:T(8,128)(2,1)S(1)} %pad_maximum_fusion.5), channel_id=1, source_target_pairs={{4,0},{8,4},{12,8},{5,1},{9,5},{13,9},{6,2},{10,6},{14,10},{7,3},{... | collective-permute-start | bytes 1572872 | tf_op jit(solution)/shard_map/ppermute | solution.py:29
  270.0 47.2 %collective-permute-start.6 = (bf16[2,512,256]{2,1,0:T(8,128)(2,1)S(1)}, bf16[2,512,256]{2,1,0:T(8,128)(2,1)S(1)}, u32[]{:S(2)}, u32[]{:S(2)}) collective-permute-start(bf16[2,512,256]{2,1,0:T(8,128)(2,1)S(1)} %pad_maximum_fusion.5), channel_id=1, source_target_pairs={{8,0},{12,4},{9,1},{13,5},{10,2},{14,6},{11,3},{15,7},{24,16},{28,... | collective-permute-start | bytes 1572872 | tf_op jit(solution)/shard_map/ppermute | solution.py:29
  273.5 43.7 %collective-permute-start.7 = (bf16[2,512,256]{2,1,0:T(8,128)(2,1)S(1)}, bf16[2,512,256]{2,1,0:T(8,128)(2,1)S(1)}, u32[]{:S(2)}, u32[]{:S(2)}) collective-permute-start(bf16[2,512,256]{2,1,0:T(8,128)(2,1)S(1)} %pad_maximum_fusion.5), channel_id=1, source_target_pairs={{12,0},{13,1},{14,2},{15,3},{28,16},{29,17},{30,18},{31,19}} | collective-permute-start | bytes 1572872 | tf_op jit(solution)/shard_map/ppermute | solution.py:29
  411.3 37.4 %copy-start.8 = (bf16[512,1024]{1,0:T(8,128)(2,1)S(1)}, bf16[512,1024]{1,0:T(8,128)(2,1)}, u32[]{:S(2)}) copy-start(bf16[512,1024]{1,0:T(8,128)(2,1)} %param.22) | copy-start | bytes 3145732
  413.9 82.4 %all-gather.12.cloned.1.call-start = ((), (), s32[]{:S(2)}) async-start(), calls=%async_computation.6 | async-start | bytes 2621440 | tf_op jit(solution)/shard_map/all_gather | solution.py:238
  414.5 128.3 %all-gather.14.cloned.1.call-start = ((), (), s32[]{:S(2)}) async-start(), calls=%async_computation.7 | async-start | bytes 2621440 | tf_op jit(solution)/shard_map/all_gather | solution.py:241
  415.1 171.9 %all-reduce.9.cloned.1.call-start = ((), (), s32[]{:S(2)}) async-start(), calls=%async_computation.8 | async-start | bytes 2097152 | tf_op jit(solution)/shard_map/psum | solution.py:242
  552.4 73.7 %all-gather.6.cloned.1.call-start = ((), (), s32[]{:S(2)}) async-start(), calls=%async_computation.1 | async-start | bytes 1966080 | tf_op jit(solution)/shard_map/all_gather | solution.py:247
  553.1 180.3 %reduce-scatter.2.cloned.1.call-start = ((), (), s32[]{:S(2)}) async-start(), calls=%async_computation.9 | async-start | bytes 1310720 | tf_op jit(solution)/shard_map/reduce_scatter | solution.py:268
  627.6 6.9 copy-start.21
  627.6 32.2 %copy-start.14 = (bf16[512,1024]{1,0:T(8,128)(2,1)S(1)}, bf16[512,1024]{1,0:T(8,128)(2,1)}, u32[]{:S(2)}) copy-start(bf16[512,1024]{1,0:T(8,128)(2,1)} %param.21) | copy-start | bytes 3145732
  629.3 32.1 %collective-permute-start.8 = (bf16[2,512,256]{2,1,0:T(8,128)(2,1)S(1)}, bf16[2,512,256]{2,1,0:T(8,128)(2,1)S(1)}, u32[]{:S(2)}, u32[]{:S(2)}) collective-permute-start(bf16[2,512,256]{2,1,0:T(8,128)(2,1)S(1)} %pad_maximum_fusion.6), channel_id=1, source_target_pairs={{0,4},{4,8},{8,12},{1,5},{5,9},{9,13},{2,6},{6,10},{10,14},{3,7},{... | collective-permute-start | bytes 1572872 | tf_op jit(solution)/shard_map/ppermute | solution.py:18
  631.8 29.5 %collective-permute-start.9 = (bf16[2,512,256]{2,1,0:T(8,128)(2,1)S(1)}, bf16[2,512,256]{2,1,0:T(8,128)(2,1)S(1)}, u32[]{:S(2)}, u32[]{:S(2)}) collective-permute-start(bf16[2,512,256]{2,1,0:T(8,128)(2,1)S(1)} %pad_maximum_fusion.6), channel_id=1, source_target_pairs={{4,0},{8,4},{12,8},{5,1},{9,5},{13,9},{6,2},{10,6},{14,10},{7,3},{... | collective-permute-start | bytes 1572872 | tf_op jit(solution)/shard_map/ppermute | solution.py:21
  662.3 6.8 copy-start.16
  673.6 6.8 copy-start.16
  684.9 6.8 copy-start.16
  696.1 6.8 copy-start.16
  707.4 27.7 %copy-start.1 = (s32[16,8]{0,1:T(8,128)S(1)}, s32[16,8]{0,1:T(8,128)}, u32[]{:S(2)}) copy-start(s32[16,8]{0,1:T(8,128)} %param.31) | copy-start | bytes 1540
  (32 other events, 78.3 us)
Sparse Core Ops, SparseCore 0:
  8.9 42.8 all-gather.7
  137.1 35.5 all-reduce.4
  174.2 37.4 all-gather.9
  414.0 34.6 all-reduce.6
  450.1 46.1 all-gather.11
  497.7 45.0 all-gather.13
  552.5 34.4 all-reduce.8
  588.6 37.4 all-gather.5
  710.1 23.1 reduce-scatter.1
where the time goes:
time: 746 us; the launch traced here: 742 us
  waiting for transfers between devices  365 us (49%)
  matrix products  120 us (16%)
  blocking collectives  95 us (13%)
  local copies, waits for them, and re-layouts  60.9 us (8%)
  other arithmetic  41.2 us (6%)
  loops' own time  26.4 us (4%)
  starting transfers between devices  19.6 us (3%)
  between operations  13.7 us (2%)
    dot_general x48, matrix products, head_scores(): jnp.einsum('qd,kd->qk', queries[:, lower:lower + HD], key_rows[:, lower:l...  61.3 us
    all_gather x1, blocking collectives, per_device(): lax.all_gather(proc_out, 'band', axis=1, tiled=True)  47.1 us
    all_gather x1, waiting for transfers between devices, per_device(): lax.all_gather(ff_down, 'band', axis=1, tiled=True)  46.5 us
    all_gather x1, waiting for transfers between devices, per_device(): lax.all_gather(ff_up, 'band', axis=0, tiled=True)  45.2 us
    ppermute x6, waiting for transfers between devices, shifted(): return lax.ppermute(block, axis, route)  41 us
    all_gather x1, waiting for transfers between devices, per_device(): lax.all_gather(dec_in, 'band', axis=1, tiled=True)  36.6 us
    all_gather x1, waiting for transfers between devices, per_device(): lax.all_gather(proc_in, 'band', axis=1, tiled=True)  36.5 us
    psum x1, waiting for transfers between devices, per_device(): lax.psum(enc_terms.astype(jnp.bfloat16), 'head').astype(jnp.float32)  34.9 us
  transfers between devices with their start and end apart: 19, of which 14 were waited for; matrix products, arithmetic and copies ran while one was open for 3% of the time, Pallas kernels for 0%

commit v1 on v0

--- a/solution.py
+++ b/solution.py
@@ -8,6 +8,27 @@
 WINDOW = 1536
 EPSILON = 1e-05
 NEGATIVE = -1e30
+
+
+def joined_along(blocks, dim):
+    blocks = jnp.moveaxis(blocks, 0, dim)
+    shape = blocks.shape
+    return blocks.reshape(*shape[:dim], shape[dim] * shape[dim + 1], *shape[dim + 2 :])
+
+
+def grow_blocks(value, axis):
+    devices, index = (lax.axis_size(axis), lax.axis_index(axis))
+    blocks, bit = (value[None], 1)
+    while bit < devices:
+        other = lax.ppermute(blocks, axis, [(i, i ^ bit) for i in range(devices)])
+        low = index & bit == 0
+        blocks = jnp.concatenate([jnp.where(low, blocks, other), jnp.where(low, other, blocks)])
+        bit *= 2
+    return blocks
+
+
+def doubled_up(x, axis, dim):
+    return joined_along(grow_blocks(x, axis), dim)
 
 
 def padded(block, sides, width):
@@ -238,7 +259,7 @@
         lax.all_gather(ff_up, "band", axis=0, tiled=True),
     )
     hidden = jax.nn.gelu(hidden, approximate=False).astype(jnp.bfloat16)
-    ff_terms = columns_of(hidden, lax.all_gather(ff_down, "band", axis=1, tiled=True))
+    ff_terms = columns_of(hidden, doubled_up(ff_down, "band", 1))
     mesh_final = mesh_mid + lax.psum(ff_terms.astype(jnp.bfloat16), "head").astype(jnp.float32)
     final_norm = normed(mesh_final)
     dec_q, dec_k, dec_v = fold_three(

time: 746 us -> 709 us (0.950)
  waiting for transfers between devices: 365 us -> 326 us
    ppermute x0 -> x2, waiting for transfers between devices: none -> 79.8 us  [grow_blocks(): other = lax.ppermute(blocks, axis, [(i, i ^ bit) for i in range(devices)])]
    all_gather x1 -> x0, waiting for transfers between devices: 46.5 us -> none  [per_device(): lax.all_gather(ff_down, 'band', axis=1, tiled=True)]
    all_gather x1, waiting for transfers between devices: 45.2 us -> 6.65 us  [per_device(): lax.all_gather(ff_up, 'band', axis=0, tiled=True)]
    psum x1, waiting for transfers between devices: 33.3 us -> 0.01 us  [per_device(): lax.psum(proc_terms.astype(jnp.bfloat16), 'head').astype(jnp.float32)]
  transfers between devices with their start and end apart: 19 -> 20, of which waited for: 14 -> 14; matrix products, arithmetic and copies ran while one was open for 3% -> 3% of each run, Pallas kernels for 0% -> 0%
where the time goes in v1:
time: 709 us; the launch traced here: 705 us
  waiting for transfers between devices  326 us (46%)
  matrix products  120 us (17%)
  blocking collectives  95 us (13%)
  local copies, waits for them, and re-layouts  61.1 us (9%)
  other arithmetic  43 us (6%)
  loops' own time  26.4 us (4%)
  starting transfers between devices  19.7 us (3%)
  between operations  14 us (2%)
    ppermute x2, waiting for transfers between devices, grow_blocks(): other = lax.ppermute(blocks, axis, [(i, i ^ bit) for i in range(devices)])  79.8 us
    dot_general x48, matrix products, head_scores(): jnp.einsum('qd,kd->qk', queries[:, lower:lower + HD], key_rows[:, lower:l...  61.3 us
    all_gather x1, blocking collectives, per_device(): lax.all_gather(proc_out, 'band', axis=1, tiled=True)  47.1 us
    ppermute x6, waiting for transfers between devices, shifted(): return lax.ppermute(block, axis, route)  41 us
    all_gather x1, waiting for transfers between devices, per_device(): lax.all_gather(dec_in, 'band', axis=1, tiled=True)  36.6 us
    all_gather x1, waiting for transfers between devices, per_device(): lax.all_gather(proc_in, 'band', axis=1, tiled=True)  36.5 us
    psum x1, waiting for transfers between devices, per_device(): lax.psum(enc_terms.astype(jnp.bfloat16), 'head').astype(jnp.float32)  34.9 us
    psum x1, waiting for transfers between devices, per_device(): lax.psum(ff_terms.astype(jnp.bfloat16), 'head').astype(jnp.float32)  33.9 us
  transfers between devices with their start and end apart: 20, of which 14 were waited for; matrix products, arithmetic and copies ran while one was open for 3% of the time, Pallas kernels for 0%

profile of v1, /device:TPU:0, one launch (start us, length us, event | category | flops | bytes accessed | tf_op | source)
XLA Modules:
  0.0 704.9 jit_solution(4690798008039495448)
XLA Ops:
  9.9 22.7 %all_gather.23 = bf16[256,1024]{1,0:T(8,128)(2,1)} all-gather(bf16[256,256]{1,0:T(8,128)(2,1)S(1)} %copy-done.20), channel_id=1, replica_groups=mesh['members'=2,'band'=4,'head'=4] {'band'}, dimensions={1}, use_global_device_ids=true | all-gather | bytes 655360 | tf_op jit(solution)/shard_map/all_gather | solution.py:211
  32.6 19.2 %all-gather.7.cloned.1.call-done = bf16[3,1024,256]{2,1,0:T(8,128)(2,1)} async-done(((bf16[3,256,256]{2,1,0:T(8,128)(2,1)}), bf16[3,1024,256]{2,1,0:T(8,128)(2,1)}) %all-gather.7.cloned.1.call-update) | async-done | bytes 1572880 | tf_op jit(solution)/shard_map/all_gather | solution.py:199
  54.9 3.3 collective-permute-start
  62.0 7.4 %collective-permute-done = bf16[2,512,256]{2,1,0:T(8,128)(2,1)S(1)} collective-permute-done((bf16[2,512,256]{2,1,0:T(8,128)(2,1)S(1)}, bf16[2,512,256]{2,1,0:T(8,128)(2,1)S(1)}, u32[]{:S(2)}, u32[]{:S(2)}) %collective-permute-start) | collective-permute-done | bytes 524320 | tf_op jit(solution)/shard_map/ppermute | solution.py:39
  69.4 4.1 collective-permute-done.1
  74.6 59.4 %while.34 = (s32[]{:T(128)}, f32[4,128,256]{2,1,0:T(8,128)}, f32[4,128,4]{1,2,0:T(4,128)S(1)}, s32[4]{0:T(128)S(1)}, s32[4,8]{1,0:T(4,128)S(1)}, /*index=5*/s32[...) while((s32[]{:T(128)}, f32[4,128,256]{2,1,0:T(8,128)}, ...), condition=%wide.region_13.14_spmd, body=%wide.region_4.13_spmd.sunk | while | flops 474056288 | bytes 11562037 | solution.py:158
  137.8 34.9 %all-reduce.5.cloned.1.call-done = bf16[512,1024]{1,0:T(8,128)(2,1)} async-done(((bf16[512,1024]{1,0:T(8,128)(2,1)}), bf16[512,1024]{1,0:T(8,128)(2,1)}) %all-reduce.5.cloned.1.call-update) | async-done | bytes 1048592 | tf_op jit(solution)/shard_map/psum | solution.py:212
  175.3 36.5 %all-gather.9.cloned.1.call-done = bf16[3,1024,256]{2,1,0:T(8,128)(2,1)} async-done(((bf16[3,256,256]{2,1,0:T(8,128)(2,1)}), bf16[3,1024,256]{2,1,0:T(8,128)(2,1)}) %all-gather.9.cloned.1.call-update) | async-done | bytes 1572880 | tf_op jit(solution)/shard_map/all_gather | solution.py:219
  214.9 3.2 collective-permute-start.2
  219.4 47.1 %all_gather.25 = bf16[256,1024]{1,0:T(8,128)(2,1)} all-gather(bf16[256,256]{1,0:T(8,128)(2,1)S(1)} %copy-done.21), channel_id=1, replica_groups=mesh['members'=2,'band'=4,'head'=4] {'band'}, dimensions={1}, use_global_device_ids=true | all-gather | bytes 655360 | tf_op jit(solution)/shard_map/all_gather | solution.py:253
  275.1 2.8 collective-permute-done.4
  279.0 4.5 collective-permute-done.5
  283.5 33.7 %collective-permute-done.6 = bf16[2,512,256]{2,1,0:T(8,128)(2,1)S(1)} collective-permute-done((bf16[2,512,256]{2,1,0:T(8,128)(2,1)S(1)}, bf16[2,512,256]{2,1,0:T(8,128)(2,1)S(1)}, u32[]{:S(2)}, u32[]{:S(2)}) %collective-permute-start.6) | collective-permute-done | bytes 524320 | tf_op jit(solution)/shard_map/ppermute | solution.py:50
  319.1 92.2 %while.35 = (s32[]{:T(128)}, bf16[4,128,256]{2,1,0:T(8,128)(2,1)S(1)}, s32[4]{0:T(128)S(1)}, s32[]{:T(128)}, s32[2048]{0:T(1024)S(1)}, /*index=5*/s32[]{:T(128)}...) while((s32[]{:T(128)}, ...), condition=%wide.region_27.28_spmd, body=%wide.region_17.27_spmd.sunk | while | flops 422220800 | bytes 58421236 | solution.py:250
  334.7 3.4 fusion.299
  351.5 2.5 fusion.298
  357.8 3.4 fusion.299
  374.6 2.5 fusion.298
  380.9 3.4 fusion.299
  403.9 3.4 fusion.299
  411.3 2.6 convolution_convert_fusion.10
  414.8 10.9 %collective-permute-done.8 = bf16[1,1024,256]{1,2,0:T(8,128)(2,1)S(1)} collective-permute-done((bf16[1,1024,256]{1,2,0:T(8,128)(2,1)S(1)}, bf16[1,1024,256]{1,2,0:T(8,128)(2,1)S(1)}, u32[]{:S(2)}, u32[]{:S(2)}) %collective-permute-start.8) | collective-permute-done | bytes 524320 | tf_op jit(solution)/shard_map/ppermute | solution.py:23
  425.9 68.8 %collective-permute-done.9 = bf16[2,1024,256]{1,2,0:T(8,128)(2,1)S(1)} collective-permute-done((bf16[2,1024,256]{1,2,0:T(8,128)(2,1)S(1)}, bf16[2,1024,256]{1,2,0:T(8,128)(2,1)S(1)}, u32[]{:S(2)}, u32[]{:S(2)}) %collective-permute-start.9) | collective-permute-done | bytes 1048608 | tf_op jit(solution)/shard_map/ppermute | solution.py:23
  498.9 6.7 all-gather.11.cloned.1.call-done
  505.5 9.6 %convolution_convert_fusion.9 = bf16[512,1024]{1,0:T(8,128)(2,1)} fusion(bf16[1024,1024]{0,1:T(8,128)(2,1)} %bitcast.212, bf16[1024,1024]{1,0:T(8,128)(2,1)} %all-gather.11.cloned.1.call-done, f32[512,1024]{1,0:T(8,128)S(1)} %get-tuple-element.283, f32[512]{0:T(512)S(1)} %add_rsqrt_fusion.1, f32[512]{0:T(512)S(1)} %broadcast_multiply_fusion.1), kind=kOutput, calls=%fused_computation.217 | convolution fusion | flops 2183659520 | bytes 7344128 | tf_op jit(solution)/shard_map/dot_general | solution.py:84
  515.9 33.9 %all-reduce.9.cloned.1.call-done = bf16[512,1024]{1,0:T(8,128)(2,1)} async-done(((bf16[512,1024]{1,0:T(8,128)(2,1)}), bf16[512,1024]{1,0:T(8,128)(2,1)}) %all-reduce.9.cloned.1.call-update) | async-done | bytes 1048592 | tf_op jit(solution)/shard_map/psum | solution.py:263
  552.3 36.6 %all-gather.5.cloned.1.call-done = bf16[3,1024,256]{2,1,0:T(8,128)(2,1)} async-done(((bf16[3,256,256]{2,1,0:T(8,128)(2,1)}), bf16[3,1024,256]{2,1,0:T(8,128)(2,1)}) %all-gather.5.cloned.1.call-update) | async-done | bytes 1572880 | tf_op jit(solution)/shard_map/all_gather | solution.py:268
  592.1 2.5 collective-permute-start.10
  597.3 25.3 %all_gather.27 = bf16[256,1024]{1,0:T(8,128)(2,1)} all-gather(bf16[256,256]{1,0:T(8,128)(2,1)S(1)} %copy-done.22), channel_id=1, replica_groups=mesh['members'=2,'band'=4,'head'=4] {'band'}, dimensions={1}, use_global_device_ids=true | all-gather | bytes 655360 | tf_op jit(solution)/shard_map/all_gather | solution.py:287
  625.1 45.1 %while.36 = (s32[]{:T(128)}, bf16[4,128,256]{2,1,0:T(8,128)(2,1)}, s32[4]{0:T(128)S(1)}, s32[4,8]{1,0:T(4,128)S(1)}, s32[]{:T(128)}, /*index=5*/s32[4]{0:T(128)}...) while((s32[]{:T(128)}, bf16[4,128,256]{2,1,0:T(8,128)(2,1)}, ...), condition=%wide.region_43.44_spmd, body=%wide.region_34.43_spmd.sunk | while | flops 139755616 | bytes 19489944 | solution.py:158
  670.2 2.6 convolution_convert_fusion.8
  672.8 23.4 %reduce-scatter.2.cloned.1.call-done = bf16[128,1024]{1,0:T(8,128)(2,1)} async-done(((bf16[512,1024]{1,0:T(8,128)(2,1)}), bf16[128,1024]{1,0:T(8,128)(2,1)}) %reduce-scatter.2.cloned.1.call-update) | async-done | bytes 262160 | tf_op jit(solution)/shard_map/reduce_scatter | solution.py:289
  (426 shorter events, 204.0 us)
Async XLA Ops:
  6.5 53.0 %copy-start = (s32[16,8]{0,1:T(8,128)S(1)}, s32[16,8]{0,1:T(8,128)}, u32[]{:S(2)}) copy-start(s32[16,8]{0,1:T(8,128)} %param.31) | copy-start | bytes 1540
  6.5 45.2 %all-gather.7.cloned.1.call-start = ((), (), s32[]{:S(2)}) async-start(), calls=%async_computation.2 | async-start | bytes 1966080 | tf_op jit(solution)/shard_map/all_gather | solution.py:199
  7.3 165.4 %all-reduce.5.cloned.1.call-start = ((), (), s32[]{:S(2)}) async-start(), calls=%async_computation.3 | async-start | bytes 2097152 | tf_op jit(solution)/shard_map/psum | solution.py:212
  53.3 6.4 copy-start.24
  54.9 14.5 %collective-permute-start = (bf16[2,512,256]{2,1,0:T(8,128)(2,1)S(1)}, bf16[2,512,256]{2,1,0:T(8,128)(2,1)S(1)}, u32[]{:S(2)}, u32[]{:S(2)}) collective-permute-start(bf16[2,512,256]{2,1,0:T(8,128)(2,1)S(1)} %pad_maximum_fusion.6), channel_id=1, source_target_pairs={{0,4},{4,8},{8,12},{1,5},{5,9},{9,13},{2,6},{6,10},{10,14},{3,7},{... | collective-permute-start | bytes 1572872 | tf_op jit(solution)/shard_map/ppermute | solution.py:39
  58.2 15.3 %collective-permute-start.1 = (bf16[2,512,256]{2,1,0:T(8,128)(2,1)S(1)}, bf16[2,512,256]{2,1,0:T(8,128)(2,1)S(1)}, u32[]{:S(2)}, u32[]{:S(2)}) collective-permute-start(bf16[2,512,256]{2,1,0:T(8,128)(2,1)S(1)} %pad_maximum_fusion.6), channel_id=1, source_target_pairs={{4,0},{8,4},{12,8},{5,1},{9,5},{13,9},{6,2},{10,6},{14,10},{7,3},{... | collective-permute-start | bytes 1572872 | tf_op jit(solution)/shard_map/ppermute | solution.py:42
  134.3 38.4 %copy-start.7 = (bf16[512,1024]{1,0:T(8,128)(2,1)S(1)}, bf16[512,1024]{1,0:T(8,128)(2,1)}, u32[]{:S(2)}) copy-start(bf16[512,1024]{1,0:T(8,128)(2,1)} %param.22) | copy-start | bytes 3145732
  137.0 74.8 %all-gather.9.cloned.1.call-start = ((), (), s32[]{:S(2)}) async-start(), calls=%async_computation.4 | async-start | bytes 1966080 | tf_op jit(solution)/shard_map/all_gather | solution.py:219
  137.7 358.7 %all-reduce.7.cloned.1.call-start = ((), (), s32[]{:S(2)}) async-start(), calls=%async_computation.5 | async-start | bytes 2097152 | tf_op jit(solution)/shard_map/psum | solution.py:254
  213.3 6.2 copy-start.21
  213.3 55.4 %copy-start.19 = (s32[2048]{0:T(1024)S(1)}, s32[2048]{0:T(1024)}, u32[]{:S(2)}) copy-start(s32[2048]{0:T(1024)} %param.35) | copy-start | bytes 24580
  214.9 58.6 %collective-permute-start.2 = (bf16[2,512,256]{2,1,0:T(8,128)(2,1)S(1)}, bf16[2,512,256]{2,1,0:T(8,128)(2,1)S(1)}, u32[]{:S(2)}, u32[]{:S(2)}) collective-permute-start(bf16[2,512,256]{2,1,0:T(8,128)(2,1)S(1)} %pad_maximum_fusion.7), channel_id=1, source_target_pairs={{0,12},{1,13},{2,14},{3,15},{16,28},{17,29},{18,30},{19,31}} | collective-permute-start | bytes 1572872 | tf_op jit(solution)/shard_map/ppermute | solution.py:50
  218.1 56.9 %collective-permute-start.3 = (bf16[2,512,256]{2,1,0:T(8,128)(2,1)S(1)}, bf16[2,512,256]{2,1,0:T(8,128)(2,1)S(1)}, u32[]{:S(2)}, u32[]{:S(2)}) collective-permute-start(bf16[2,512,256]{2,1,0:T(8,128)(2,1)S(1)} %pad_maximum_fusion.7), channel_id=1, source_target_pairs={{0,8},{4,12},{1,9},{5,13},{2,10},{6,14},{3,11},{7,15},{16,24},{20,... | collective-permute-start | bytes 1572872 | tf_op jit(solution)/shard_map/ppermute | solution.py:50
  266.5 11.3 %collective-permute-start.4 = (bf16[2,512,256]{2,1,0:T(8,128)(2,1)S(1)}, bf16[2,512,256]{2,1,0:T(8,128)(2,1)}, u32[]{:S(2)}, u32[]{:S(2)}) collective-permute-start(bf16[2,512,256]{2,1,0:T(8,128)(2,1)S(1)} %pad_maximum_fusion.7), channel_id=1, source_target_pairs={{0,4},{4,8},{8,12},{1,5},{5,9},{9,13},{2,6},{6,10},{10,14},{3,7},{... | collective-permute-start | bytes 1572872 | tf_op jit(solution)/shard_map/ppermute | solution.py:50
  268.7 14.7 %collective-permute-start.5 = (bf16[2,512,256]{2,1,0:T(8,128)(2,1)S(1)}, bf16[2,512,256]{2,1,0:T(8,128)(2,1)S(1)}, u32[]{:S(2)}, u32[]{:S(2)}) collective-permute-start(bf16[2,512,256]{2,1,0:T(8,128)(2,1)S(1)} %pad_maximum_fusion.7), channel_id=1, source_target_pairs={{4,0},{8,4},{12,8},{5,1},{9,5},{13,9},{6,2},{10,6},{14,10},{7,3},{... | collective-permute-start | bytes 1572872 | tf_op jit(solution)/shard_map/ppermute | solution.py:50
  270.0 47.2 %collective-permute-start.6 = (bf16[2,512,256]{2,1,0:T(8,128)(2,1)S(1)}, bf16[2,512,256]{2,1,0:T(8,128)(2,1)S(1)}, u32[]{:S(2)}, u32[]{:S(2)}) collective-permute-start(bf16[2,512,256]{2,1,0:T(8,128)(2,1)S(1)} %pad_maximum_fusion.7), channel_id=1, source_target_pairs={{8,0},{12,4},{9,1},{13,5},{10,2},{14,6},{11,3},{15,7},{24,16},{28,... | collective-permute-start | bytes 1572872 | tf_op jit(solution)/shard_map/ppermute | solution.py:50
  273.5 43.7 %collective-permute-start.7 = (bf16[2,512,256]{2,1,0:T(8,128)(2,1)S(1)}, bf16[2,512,256]{2,1,0:T(8,128)(2,1)S(1)}, u32[]{:S(2)}, u32[]{:S(2)}) collective-permute-start(bf16[2,512,256]{2,1,0:T(8,128)(2,1)S(1)} %pad_maximum_fusion.7), channel_id=1, source_target_pairs={{12,0},{13,1},{14,2},{15,3},{28,16},{29,17},{30,18},{31,19}} | collective-permute-start | bytes 1572872 | tf_op jit(solution)/shard_map/ppermute | solution.py:50
  413.9 91.6 %all-gather.11.cloned.1.call-start = ((), (), s32[]{:S(2)}) async-start(), calls=%async_computation.6 | async-start | bytes 2621440 | tf_op jit(solution)/shard_map/all_gather | solution.py:259
  414.2 11.5 %collective-permute-start.8 = (bf16[1,1024,256]{1,2,0:T(8,128)(2,1)S(1)}, bf16[1,1024,256]{1,2,0:T(8,128)(2,1)S(1)}, u32[]{:S(2)}, u32[]{:S(2)}) collective-permute-start(bf16[1,1024,256]{1,2,0:T(8,128)(2,1)S(1)} %bitcast.211), channel_id=1, source_target_pairs={{0,4},{4,0},{8,12},{12,8},{1,5},{5,1},{9,13},{13,9},{2,6},{6,2},{1... | collective-permute-start | bytes 1572872 | tf_op jit(solution)/shard_map/ppermute | solution.py:23
  414.5 135.3 %all-reduce.9.cloned.1.call-start = ((), (), s32[]{:S(2)}) async-start(), calls=%async_computation.7 | async-start | bytes 2097152 | tf_op jit(solution)/shard_map/psum | solution.py:263
  425.9 68.9 %collective-permute-start.9 = (bf16[2,1024,256]{1,2,0:T(8,128)(2,1)S(1)}, bf16[2,1024,256]{1,2,0:T(8,128)(2,1)S(1)}, u32[]{:S(2)}, u32[]{:S(2)}) collective-permute-start(bf16[2,1024,256]{1,2,0:T(8,128)(2,1)S(1)} %pad_maximum_fusion.5), channel_id=1, source_target_pairs={{0,8},{4,12},{8,0},{12,4},{1,9},{5,13},{9,1},{13,5},{2,10},{6,14},... | collective-permute-start | bytes 3145736 | tf_op jit(solution)/shard_map/ppermute | solution.py:23
  515.1 73.8 %all-gather.5.cloned.1.call-start = ((), (), s32[]{:S(2)}) async-start(), calls=%async_computation.1 | async-start | bytes 1966080 | tf_op jit(solution)/shard_map/all_gather | solution.py:268
  515.8 180.4 %reduce-scatter.2.cloned.1.call-start = ((), (), s32[]{:S(2)}) async-start(), calls=%async_computation.8 | async-start | bytes 1310720 | tf_op jit(solution)/shard_map/reduce_scatter | solution.py:289
  590.4 6.9 copy-start.22
  590.4 32.2 %copy-start.14 = (bf16[512,1024]{1,0:T(8,128)(2,1)S(1)}, bf16[512,1024]{1,0:T(8,128)(2,1)}, u32[]{:S(2)}) copy-start(bf16[512,1024]{1,0:T(8,128)(2,1)} %param.21) | copy-start | bytes 3145732
  592.1 32.1 %collective-permute-start.10 = (bf16[2,512,256]{2,1,0:T(8,128)(2,1)S(1)}, bf16[2,512,256]{2,1,0:T(8,128)(2,1)S(1)}, u32[]{:S(2)}, u32[]{:S(2)}) collective-permute-start(bf16[2,512,256]{2,1,0:T(8,128)(2,1)S(1)} %pad_maximum_fusion.8), channel_id=1, source_target_pairs={{0,4},{4,8},{8,12},{1,5},{5,9},{9,13},{2,6},{6,10},{10,14},{3,7},{... | collective-permute-start | bytes 1572872 | tf_op jit(solution)/shard_map/ppermute | solution.py:39
  594.6 29.5 %collective-permute-start.11 = (bf16[2,512,256]{2,1,0:T(8,128)(2,1)S(1)}, bf16[2,512,256]{2,1,0:T(8,128)(2,1)S(1)}, u32[]{:S(2)}, u32[]{:S(2)}) collective-permute-start(bf16[2,512,256]{2,1,0:T(8,128)(2,1)S(1)} %pad_maximum_fusion.8), channel_id=1, source_target_pairs={{4,0},{8,4},{12,8},{5,1},{9,5},{13,9},{6,2},{10,6},{14,10},{7,3},{... | collective-permute-start | bytes 1572872 | tf_op jit(solution)/shard_map/ppermute | solution.py:42
  625.1 6.8 copy-start.16
  636.4 6.8 copy-start.16
  647.7 6.8 copy-start.16
  658.9 6.8 copy-start.16
  670.2 27.8 %copy-start.1 = (s32[16,8]{0,1:T(8,128)S(1)}, s32[16,8]{0,1:T(8,128)}, u32[]{:S(2)}) copy-start(s32[16,8]{0,1:T(8,128)} %param.31) | copy-start | bytes 1540
  (34 other events, 82.4 us)
Sparse Core Ops, SparseCore 0:
  8.9 42.8 all-gather.6
  137.1 35.5 all-reduce.4
  174.2 37.4 all-gather.8
  414.0 34.6 all-reduce.6
  450.1 55.3 all-gather.10
  515.2 34.5 all-reduce.8
  551.4 37.4 all-gather.4
  672.9 23.2 reduce-scatter.1
